TPU v7x, 32 devices: a whole 2x2x4 slice. The times are simulated.
32 devices in a mesh: section: 16 (over z, y, core), tensor: 2 (over x).
Axes of the slice: x: 2, y: 2, z: 4, core: 2. Of those that a mesh axis runs over, the one named last changes fastest.
Arguments:
- saved: bfloat16 [16, 16, 64, 8192], P('section', None, 'tensor'), may hold values from -6 to 6
- offsets: int32 [16, 16], P('section'), may hold values from 0 to 15, as said below
Outputs:
- restored: float32 [16, 16, 64, 8192], P('section', None, None, 'tensor')
- block_sums: float32 [16, 16, 8192], P('section', None, 'tensor')
Inputs may be any that keep to these rules, and one draw needn't show every extreme that they name: Each row of offsets is a permutation of 0 to 15.
All inputs are finite; a program needn't handle non-finite values.
Results may differ from a plain program's by a relative error of at most 0.0003.
Values may be sent and summed in bfloat16 or wider, within the bound.
A program may use at most 128 MiB of HBM per device.

v0:
```python
import jax
import jax.numpy as jnp
from jax import lax
from jax.sharding import PartitionSpec as P


def invert(table, count):
    return jnp.zeros((count,), jnp.int32).at[table].set(jnp.arange(count, dtype=jnp.int32))


def body(saved, offsets):
    count = lax.axis_size("section")
    mine = lax.axis_index("section")
    table = offsets[0]
    blocks = saved[0]
    order = invert((mine + table) % count, count)
    outgoing = jnp.take(blocks, order, axis=0)
    split_cols = lax.all_to_all(outgoing, "tensor", split_axis=2, concat_axis=1, tiled=True)
    arrived = lax.all_to_all(split_cols, "section", split_axis=0, concat_axis=0, tiled=True)
    restored = arrived.astype(jnp.float32)
    block_sums = jnp.sum(restored, axis=1)
    return (restored[None], block_sums[None])


def solution(mesh):
    return jax.shard_map(
        body,
        mesh=mesh,
        in_specs=(P("section", None, "tensor", None), P("section", None)),
        out_specs=(P("section", None, None, "tensor"), P("section", None, "tensor")),
        check_vma=False,
    )
```

profile of v0, /device:TPU:9, one launch (start us, length us, event | category | flops | bytes accessed | tf_op | source)
XLA Modules:
  0.0 462.3 jit_solution(6065663858853515315)
XLA Ops:
  0.6 0.7 fusion.1
  1.3 0.6 scatter_custom_fusion
  2.0 8.3 %gather_fusion = bf16[16,32,8192]{2,1,0:T(8,128)(2,1)} fusion(bf16[16,32,8192]{2,1,0:T(8,128)(2,1)} %bitcast.18, s32[1024]{0:T(1024)S(1)} %pad_clamp_fusion), kind=kCustom, calls=%fused_computation | custom fusion | bytes 16777280 | tf_op jit(solution)/shard_map/jit(_take)/gather | solution.py:17
  10.3 7.6 %broadcast_select_fusion = bf16[16,32,8192]{2,1,0:T(8,128)(2,1)} fusion(bf16[16,32,8192]{2,1,0:T(8,128)(2,1)} %gather_fusion, pred[16]{0:T(512)(128)(4,1)S(1)} %compare_and_fusion), kind=kLoop, calls=%fused_computation.4 | loop fusion | flops 4194304 | bytes 16777232 | tf_op jit(solution)/shard_map/jit(_take)/select_n | solution.py:17
  17.9 34.7 %copy.6 = bf16[16,32,8192]{1,0,2:T(8,128)(2,1)} copy(bf16[16,32,8192]{2,1,0:T(8,128)(2,1)} %broadcast_select_fusion) | data formatting | bytes 16777216 | tf_op jit(solution)/shard_map/jit(_take)/select_n | solution.py:17
  52.6 27.6 %reshape.82 = bf16[2,2,1048576]{2,1,0:T(2,128)(2,1)} reshape(bf16[8192,16,32]{2,1,0:T(8,128)(2,1)} %bitcast.15) | data formatting | bytes 16777216
  80.2 102.8 %all_to_all.23 = bf16[2,2,1048576]{2,1,0:T(2,128)(2,1)} all-to-all(bf16[2,2,1048576]{2,1,0:T(2,128)(2,1)} %reshape.82), channel_id=1, replica_groups=mesh['section'=16,'tensor'=2] {'tensor'}, dimensions={0} | all-to-all | bytes 16777216 | tf_op jit(solution)/shard_map/all_to_all | solution.py:18
  183.0 38.0 %reshape.83 = bf16[8192,16,32]{2,1,0:T(8,128)(2,1)} reshape(bf16[2,2,1048576]{2,1,0:T(2,128)(2,1)} %all_to_all.23) | data formatting | bytes 16777216
  221.0 33.7 %copy.7 = bf16[16,2,32,4096]{3,2,1,0:T(8,128)(2,1)} copy(bf16[16,2,32,4096]{2,0,3,1:T(8,128)(2,1)} %bitcast.16) | data formatting | bytes 16777216 | tf_op jit(solution)/shard_map/all_to_all | solution.py:18
  254.7 190.1 %all_to_all.24 = bf16[16,64,4096]{2,1,0:T(8,128)(2,1)S(1)} all-to-all(bf16[16,64,4096]{2,1,0:T(8,128)(2,1)} %bitcast.17), channel_id=1, replica_groups=mesh['section'=16,'tensor'=2] {'section'}, dimensions={0} | all-to-all | bytes 16777216 | tf_op jit(solution)/shard_map/all_to_all | solution.py:19
  444.8 0.0 copy-start
  444.8 3.2 copy-done
  448.0 2.4 convert_reduce_fusion
  450.5 11.8 %convert_bitcast_fusion = f32[1,16,64,4096]{3,2,1,0:T(8,128)} fusion(bf16[16,64,4096]{2,1,0:T(8,128)(2,1)} %copy-done), kind=kLoop, calls=%fused_computation.3 | loop fusion | flops 4194304 | bytes 25165824 | tf_op jit(solution)/shard_map/broadcast_in_dim | solution.py:22
  (4 shorter events, 0.0 us)
Async XLA Ops:
  444.8 3.2 copy-start
where the time goes:
time: 465 us; the launch traced here: 462 us
  blocking collectives  293 us (63%)
  local copies, waits for them, and re-layouts  146 us (31%)
  other arithmetic  22.6 us (5%)
    all_to_all x1, blocking collectives, body(): lax.all_to_all(split_cols, 'section', split_axis=0, concat_axis=0, tiled=...  190 us
    all_to_all x1, blocking collectives, body(): lax.all_to_all(outgoing, 'tensor', split_axis=2, concat_axis=1, tiled=True)  103 us
    unnamed x4, local copies, waits for them, and re-layouts  68.8 us
    select_n x1, local copies, waits for them, and re-layouts, body(): outgoing = jnp.take(blocks, order, axis=0)  34.7 us
    all_to_all x1, local copies, waits for them, and re-layouts, body(): lax.all_to_all(outgoing, 'tensor', split_axis=2, concat_axis=1, tiled=True)  33.7 us
    broadcast_in_dim x1, other arithmetic, body(): return (restored[None], block_sums[None])  11.8 us

commit v1 on v0

v1 whole, which is shorter than its diff:
```python
import jax
import jax.numpy as jnp
from jax import lax
from jax.experimental import pallas as pl
from jax.experimental.pallas import tpu as pltpu
from jax.sharding import PartitionSpec as P

MESH = pl.DeviceIdType.MESH


def partner(index, step, count):
    if count & (count - 1):
        return (index + step) % count
    other = index
    bit = 1
    while bit < count:
        if step & bit:
            other = other + bit * (1 - 2 * ((index // bit) % 2))
        bit *= 2
    return other


def send_order(n, m):
    far = [(k, e) for k in range(n // 2, n) for e in range(m)]
    near = [(k, e) for k in range(n // 2 - 1, -1, -1) for e in range(m)]
    mixed = []
    for i in range(max(len(far), len(near))):
        mixed += far[i : i + 1] + near[i : i + 1]
    return mixed


def exchange(n, m, offsets, saved, arrived, held, out_box, load_sem, send_sem, recv_sem, own_sem):
    s = lax.axis_index("section")
    x = lax.axis_index("tensor")
    rows = saved.shape[1]
    cols = saved.shape[2] // m
    load = pltpu.make_async_copy(saved, held, load_sem)
    load.start()

    barrier = pltpu.get_barrier_semaphore()

    def greet(i, carry):
        j = i + 1
        pl.semaphore_signal(
            barrier,
            inc=1,
            device_id=((s + j // m) % n, (x + j % m) % m),
            device_id_type=MESH,
        )
        return carry

    lax.fori_loop(0, n * m - 1, greet, 0)
    load.wait()
    greeted = [False]

    def send(k, e):
        t = partner(s, k, n)
        d = partner(x, e, m)
        dst = arrived.at[s, pl.ds(x * rows, rows), :]
        if k == 0 and e == 0:
            return pltpu.make_async_copy(out_box.at[0], dst, own_sem)
        return pltpu.make_async_remote_copy(
            src_ref=out_box.at[k * m + e],
            dst_ref=dst,
            send_sem=send_sem.at[k * m + e],
            recv_sem=recv_sem.at[k * m + e],
            device_id=(t, d),
            device_id_type=MESH,
        )

    def fill(k, e):
        t = partner(s, k, n)
        d = partner(x, e, m)
        wanted = (t - s + n) % n
        slot = jnp.int32(0)
        for j in range(n):
            slot = jnp.where(offsets[0, j] == wanted, jnp.int32(j), slot)
        step = min(cols, 512)

        def move(i, carry):
            src = pl.ds(pl.multiple_of(d * cols + i * step, step), step)
            dst = pl.ds(pl.multiple_of(i * step, step), step)
            out_box[k * m + e, :, dst] = held[slot, :, src]
            return carry

        lax.fori_loop(0, cols // step, move, 0)

    copies = []
    waiting = None
    for k, e in send_order(n, m):
        fill(k, e)
        if waiting is not None:
            if not copies:
                pl.semaphore_wait(barrier, n * m - 1)
            copy = send(*waiting)
            copy.start()
            copies.append(copy)
        waiting = (k, e)
    copy = send(*waiting)
    copy.start()
    copies.append(copy)
    for copy in copies:
        copy.wait()


def body(n, m, saved, offsets):
    _, slots, rows, width = saved.shape
    cols = width // m
    arrived = pl.pallas_call(
        lambda *refs: exchange(n, m, *refs),
        out_shape=jax.ShapeDtypeStruct((slots, rows * m, cols), saved.dtype),
        in_specs=[
            pl.BlockSpec(memory_space=pltpu.SMEM),
            pl.BlockSpec(memory_space=pl.ANY),
        ],
        out_specs=pl.BlockSpec(memory_space=pl.ANY),
        scratch_shapes=[
            pltpu.VMEM((slots, rows, width), saved.dtype),
            pltpu.VMEM((slots * m, rows, cols), saved.dtype),
            pltpu.SemaphoreType.DMA,
            pltpu.SemaphoreType.DMA((n * m,)),
            pltpu.SemaphoreType.DMA((n * m,)),
            pltpu.SemaphoreType.DMA,
        ],
        compiler_params=pltpu.CompilerParams(
            collective_id=0, has_side_effects=True, vmem_limit_bytes=48 * 2**20
        ),
        name="exchange",
    )(offsets, saved[0])
    restored = arrived.astype(jnp.float32)
    block_sums = jnp.sum(restored, axis=1)
    return (restored[None], block_sums[None])


def solution(mesh):
    n = mesh.shape["section"]
    m = mesh.shape["tensor"]
    return jax.shard_map(
        lambda saved, offsets: body(n, m, saved, offsets),
        mesh=mesh,
        in_specs=(P("section", None, "tensor", None), P("section", None)),
        out_specs=(P("section", None, None, "tensor"), P("section", None, "tensor")),
        check_vma=False,
    )
```

time: 465 us -> 208 us (0.45)
  blocking collectives: 293 us -> 0 us
  Pallas kernels: 0 us -> 189 us
  local copies, waits for them, and re-layouts: 146 us -> 0.65 us
  other arithmetic: 22.6 us -> 17.6 us
    all_to_all x2 -> x0, blocking collectives: 293 us -> none  [the longest x1 190 us: body(): lax.all_to_all(split_cols, 'section', split_axis=0, concat_axis=0, tiled=...]
    pallas_call x0 -> x1, Pallas kernels: none -> 189 us  [body(): pl.pallas_call(lambda *refs: exchange(n, m, *refs), out_shape=jax.ShapeDt...]
    unnamed x4 -> x2, local copies, waits for them, and re-layouts: 68.8 us -> 0.65 us
    select_n x1 -> x0, local copies, waits for them, and re-layouts: 34.7 us -> none  [body(): outgoing = jnp.take(blocks, order, axis=0)]
    all_to_all x1 -> x0, local copies, waits for them, and re-layouts: 33.7 us -> none  [body(): lax.all_to_all(outgoing, 'tensor', split_axis=2, concat_axis=1, tiled=True)]
    gather x1 -> x0, local copies, waits for them, and re-layouts: 8.32 us -> none  [body(): outgoing = jnp.take(blocks, order, axis=0)]
    select_n x3 -> x0, other arithmetic: 8.32 us -> none  [the longest x2 7.65 us: body(): outgoing = jnp.take(blocks, order, axis=0)]
where the time goes in v1:
time: 208 us
  Pallas kernels  189 us (91%)
  other arithmetic  17.6 us (8%)
    pallas_call x1, Pallas kernels, body(): pl.pallas_call(lambda *refs: exchange(n, m, *refs), out_shape=jax.ShapeDt...  189 us
    broadcast_in_dim x1, other arithmetic, body(): return (restored[None], block_sums[None])  11.8 us
    reduce_sum x1, other arithmetic, body(): block_sums = jnp.sum(restored, axis=1)  5.82 us

profile of v1, /device:TPU:9, one launch (start us, length us, event | category | flops | bytes accessed | tf_op | source)
XLA Modules:
  0.0 208.1 jit_solution(9372979753759785601)
XLA Ops:
  0.6 0.0 copy-start
  0.6 0.6 copy-done
  1.3 189.2 %exchange.1 = bf16[16,64,4096]{2,1,0:T(8,128)(2,1)} custom-call(s32[1,16]{1,0:T(1,128)S(1)} %copy-done, bf16[16,32,8192]{2,1,0:T(8,128)(2,1)} %bitcast.4), custom_call_target="tpu_custom_call" | custom-call | tf_op jit(solution)/shard_map/exchange/pallas_call | solution.py:109
  190.5 5.8 %convert_reduce_fusion = f32[16,4096]{1,0:T(8,128)} fusion(bf16[16,64,4096]{2,1,0:T(8,128)(2,1)} %exchange.1), kind=kLoop, calls=%fused_computation | loop fusion | flops 8323072 | bytes 8650752 | tf_op jit(solution)/shard_map/reduce_sum | solution.py:131
  196.3 11.8 %convert_bitcast_fusion = f32[1,16,64,4096]{3,2,1,0:T(8,128)} fusion(bf16[16,64,4096]{2,1,0:T(8,128)(2,1)} %exchange.1), kind=kLoop, calls=%fused_computation.1 | loop fusion | flops 4194304 | bytes 25165824 | tf_op jit(solution)/shard_map/broadcast_in_dim | solution.py:132
Async XLA Ops:
  0.6 0.7 copy-start

commit v2 on v1

--- a/solution.py
+++ b/solution.py
@@ -103,6 +103,21 @@
         copy.wait()
 
 
+def widen(arrived, restored, sums):
+    i = pl.program_id(0)
+    rows, cols = arrived.shape[1:]
+    wide = min(cols, 512)
+    for c in range(0, cols, wide):
+        here = pl.ds(c, wide)
+        total = None
+        for r in range(0, rows, 16):
+            band = pl.ds(r, min(16, rows - r))
+            part = arrived[i, band, here].astype(jnp.float32)
+            restored[0, band, here] = part
+            total = part if total is None else total + part
+        sums[pl.ds(i, 1), here] = jnp.sum(total, axis=0, keepdims=True)
+
+
 def body(n, m, saved, offsets):
     _, slots, rows, width = saved.shape
     cols = width // m
@@ -111,7 +126,7 @@
         out_shape=jax.ShapeDtypeStruct((slots, rows * m, cols), saved.dtype),
         in_specs=[
             pl.BlockSpec(memory_space=pltpu.SMEM),
-            pl.BlockSpec(memory_space=pl.ANY),
+            pl.BlockSpec(memory_space=pltpu.HBM),
         ],
         out_specs=pl.BlockSpec(memory_space=pl.ANY),
         scratch_shapes=[
@@ -123,12 +138,26 @@
             pltpu.SemaphoreType.DMA,
         ],
         compiler_params=pltpu.CompilerParams(
-            collective_id=0, has_side_effects=True, vmem_limit_bytes=48 * 2**20
+            collective_id=0, has_side_effects=True, vmem_limit_bytes=20 * 2**20
         ),
         name="exchange",
-    )(offsets, saved[0])
-    restored = arrived.astype(jnp.float32)
-    block_sums = jnp.sum(restored, axis=1)
+    )(offsets, pltpu.with_memory_space_constraint(saved[0], pltpu.HBM))
+    blocks, height = arrived.shape[:2]
+    restored, block_sums = pl.pallas_call(
+        widen,
+        grid=(blocks,),
+        out_shape=[
+            jax.ShapeDtypeStruct(arrived.shape, jnp.float32),
+            jax.ShapeDtypeStruct((blocks, cols), jnp.float32),
+        ],
+        in_specs=[pl.BlockSpec(memory_space=pltpu.VMEM)],
+        out_specs=[
+            pl.BlockSpec((1, height, cols), lambda i: (i, 0, 0)),
+            pl.BlockSpec((blocks, cols), lambda i: (0, 0)),
+        ],
+        compiler_params=pltpu.CompilerParams(vmem_limit_bytes=16 * 2**20),
+        name="widen",
+    )(arrived)
     return (restored[None], block_sums[None])
 
 

time: 208 us -> 199 us (0.957)
  other arithmetic: 17.6 us -> 0 us
  Pallas kernels: 189 us -> 198 us
    broadcast_in_dim x1 -> x0, other arithmetic: 11.8 us -> none  [body(): return (restored[None], block_sums[None])]
    pallas_call x0 -> x1, Pallas kernels: none -> 8.91 us  [body(): pl.pallas_call(widen, grid=(blocks,), out_shape=[jax.ShapeDtypeStruct(arr...]
    reduce_sum x1 -> x0, other arithmetic: 5.82 us -> none  [body(): block_sums = jnp.sum(restored, axis=1)]
where the time goes in v2:
time: 199 us
  Pallas kernels  198 us (99%)
    pallas_call x1, Pallas kernels, body(): pl.pallas_call(lambda *refs: exchange(n, m, *refs), out_shape=jax.ShapeDt...  189 us
    pallas_call x1, Pallas kernels, body(): pl.pallas_call(widen, grid=(blocks,), out_shape=[jax.ShapeDtypeStruct(arr...  8.91 us

profile of v2, /device:TPU:9, one launch (start us, length us, event | category | flops | bytes accessed | tf_op | source)
XLA Modules:
  0.0 199.2 jit_solution(4742317900749016994)
XLA Ops:
  0.6 0.0 copy-start
  0.6 0.6 copy-done
  1.3 189.0 %exchange.1.arrived = bf16[16,64,4096]{2,1,0:T(8,128)(2,1)S(1)} custom-call(s32[1,16]{1,0:T(1,128)S(1)} %copy-done, bf16[16,32,8192]{2,1,0:T(8,128)(2,1)} %bitcast.3), custom_call_target="tpu_custom_call" | custom-call | tf_op jit(solution)/shard_map/exchange/pallas_call | solution.py:124
  190.3 8.9 %widen.1 = (f32[16,64,4096]{2,1,0:T(8,128)}, f32[16,4096]{1,0:T(8,128)}) custom-call(bf16[16,64,4096]{2,1,0:T(8,128)(2,1)S(1)} %exchange.1.arrived), custom_call_target="tpu_custom_call" | custom-call | tf_op jit(solution)/shard_map/widen/pallas_call | solution.py:146
Async XLA Ops:
  0.6 0.7 copy-start

commit v3 on v2

--- a/solution.py
+++ b/solution.py
@@ -103,19 +103,29 @@
         copy.wait()
 
 
-def widen(arrived, restored, sums):
-    i = pl.program_id(0)
-    rows, cols = arrived.shape[1:]
+def widen(arrived, restored, sums, stage, stage_sem):
+    blocks, rows, cols = arrived.shape
+    depth = stage.shape[0]
     wide = min(cols, 512)
-    for c in range(0, cols, wide):
-        here = pl.ds(c, wide)
-        total = None
-        for r in range(0, rows, 16):
-            band = pl.ds(r, min(16, rows - r))
-            part = arrived[i, band, here].astype(jnp.float32)
-            restored[0, band, here] = part
-            total = part if total is None else total + part
-        sums[pl.ds(i, 1), here] = jnp.sum(total, axis=0, keepdims=True)
+    copies = []
+    for i in range(blocks):
+        slot = i % depth
+        if i >= depth:
+            copies[i - depth].wait()
+        for c in range(0, cols, wide):
+            here = pl.ds(c, wide)
+            total = None
+            for r in range(0, rows, 16):
+                band = pl.ds(r, min(16, rows - r))
+                part = arrived[i, band, here].astype(jnp.float32)
+                stage[slot, band, here] = part
+                total = part if total is None else total + part
+            sums[pl.ds(i, 1), here] = jnp.sum(total, axis=0, keepdims=True)
+        copy = pltpu.make_async_copy(stage.at[slot], restored.at[i], stage_sem.at[slot])
+        copy.start()
+        copies.append(copy)
+    for copy in copies[-depth:]:
+        copy.wait()
 
 
 def body(n, m, saved, offsets):
@@ -145,17 +155,20 @@
     blocks, height = arrived.shape[:2]
     restored, block_sums = pl.pallas_call(
         widen,
-        grid=(blocks,),
         out_shape=[
             jax.ShapeDtypeStruct(arrived.shape, jnp.float32),
             jax.ShapeDtypeStruct((blocks, cols), jnp.float32),
         ],
         in_specs=[pl.BlockSpec(memory_space=pltpu.VMEM)],
         out_specs=[
-            pl.BlockSpec((1, height, cols), lambda i: (i, 0, 0)),
-            pl.BlockSpec((blocks, cols), lambda i: (0, 0)),
+            pl.BlockSpec(memory_space=pl.ANY),
+            pl.BlockSpec(memory_space=pltpu.VMEM),
         ],
-        compiler_params=pltpu.CompilerParams(vmem_limit_bytes=16 * 2**20),
+        scratch_shapes=[
+            pltpu.VMEM((6, height, cols), jnp.float32),
+            pltpu.SemaphoreType.DMA((6,)),
+        ],
+        compiler_params=pltpu.CompilerParams(vmem_limit_bytes=20 * 2**20),
         name="widen",
     )(arrived)
     return (restored[None], block_sums[None])

time: 199 us -> 197 us (0.990)
  Pallas kernels: 198 us -> 196 us
    pallas_call x1, Pallas kernels: 8.91 us -> 6.65 us  [body(): pl.pallas_call(widen, out_shape=[jax.ShapeDtypeStruct(arrived.shape, jnp....]
where the time goes in v3:
time: 197 us
  Pallas kernels  196 us (99%)
    pallas_call x1, Pallas kernels, body(): pl.pallas_call(lambda *refs: exchange(n, m, *refs), out_shape=jax.ShapeDt...  189 us
    pallas_call x1, Pallas kernels, body(): pl.pallas_call(widen, out_shape=[jax.ShapeDtypeStruct(arrived.shape, jnp....  6.65 us

profile of v3, /device:TPU:9, one launch (start us, length us, event | category | flops | bytes accessed | tf_op | source)
XLA Modules:
  0.0 196.9 jit_solution(2348803300956169513)
XLA Ops:
  0.6 0.0 copy-start
  0.6 0.6 copy-done
  1.3 189.0 %exchange.1.arrived = bf16[16,64,4096]{2,1,0:T(8,128)(2,1)S(1)} custom-call(s32[1,16]{1,0:T(1,128)S(1)} %copy-done, bf16[16,32,8192]{2,1,0:T(8,128)(2,1)} %bitcast.3), custom_call_target="tpu_custom_call" | custom-call | tf_op jit(solution)/shard_map/exchange/pallas_call | solution.py:134
  190.3 6.7 %widen.1 = (f32[16,64,4096]{2,1,0:T(8,128)}, f32[16,4096]{1,0:T(8,128)}) custom-call(bf16[16,64,4096]{2,1,0:T(8,128)(2,1)S(1)} %exchange.1.arrived), custom_call_target="tpu_custom_call" | custom-call | tf_op jit(solution)/shard_map/widen/pallas_call | solution.py:156
Async XLA Ops:
  0.6 0.7 copy-start
